TPU v7x, 128 devices: a whole 4x4x4 slice. The times are simulated.
128 devices in a mesh: gx: 4 (over y), gy: 4 (over z_hi, core), gz: 8 (over z_lo, x).
Axes of the slice: x: 4, y: 4, z: 4 (z_hi: 2, z_lo: 2; z = z_hi * 2 + z_lo), core: 2. Of those that a mesh axis runs over, the one named last changes fastest.
Arguments:
- volume: bfloat16 [32, 32, 32, 32, 128], P('gx', 'gy', 'gz'), may hold values from -6 to 6
- conv_kernel: bfloat16 [3, 3, 3, 32, 64], replicated, may hold values from -0.21875 to 0.21875
- dense_one: bfloat16 [16, 16, 16, 64, 2048], P('gx', None, None, ('gy', 'gz')), may hold values from -0.01171875 to 0.01171875
- dense_two: float32 [2048, 256], replicated, may hold values from -0.125 to 0.125
- dense_three: float32 [256, 4], replicated, may hold values from -0.375 to 0.375
- targets: float32 [4, 128], replicated, may hold values from -3 to 3
Outputs:
- prediction: float32 [4, 128], replicated
- grad_dense_one: bfloat16 [16, 16, 16, 64, 2048], P('gx', None, None, ('gy', 'gz'))
- grad_conv: float32 [3, 3, 3, 32, 64], replicated
- grad_volume: bfloat16 [32, 32, 32, 32, 128], P('gx', 'gy', 'gz')
All inputs are finite; a program needn't handle non-finite values.
Results may differ from a plain program's by a relative error of at most 0.008.
Values may be sent and summed in bfloat16 or wider, within the bound.
A program may use at most 128 MiB of HBM per device.

v0:
```python
import jax
import jax.numpy as jnp
from jax import lax
from jax.sharding import PartitionSpec as P

loss_scale = 1024.0
leak_slope = 0.3


def with_halo(array, sides, width):
    for axis, dim in sides:
        size, length = (lax.axis_size(axis), array.shape[dim])
        up = [(i, (i + 1) % size) for i in range(size - 1)]
        down = [(j, i) for i, j in up]
        last = lax.slice_in_dim(array, length - width, length, axis=dim)
        initial = lax.slice_in_dim(array, 0, width, axis=dim)
        before = lax.ppermute(last, axis, up)
        after = lax.ppermute(initial, axis, down)
        array = jnp.concatenate([before, array, after], axis=dim)
    return array


def from_behind(block, axis, distance):
    devices = range(lax.axis_size(axis))
    route = [(i - distance, i) for i in devices if i - distance in devices]
    return lax.ppermute(block, axis, route)


def shortened(array):
    return jax.tree.map(lambda a: a.astype(jnp.bfloat16) if a.dtype == jnp.float32 else a, array)


def smooth_leaky(values):
    return leak_slope * values + (1.0 - leak_slope) * jax.nn.softplus(values)


def leaky_derivative(values):
    return leak_slope + (1.0 - leak_slope) * jax.nn.sigmoid(values)


def conv_forward(padded, kernel):
    return lax.conv_general_dilated(
        padded,
        kernel,
        (1, 1, 1),
        "VALID",
        dimension_numbers=("DHWCN", "DHWIO", "DHWCN"),
        preferred_element_type=jnp.float32,
    )


def conv_back_input(padded_grad, kernel):
    flipped = kernel[::-1, ::-1, ::-1]
    return lax.conv_general_dilated(
        padded_grad,
        flipped,
        (1, 1, 1),
        "VALID",
        dimension_numbers=("DHWCN", "DHWOI", "DHWCN"),
        preferred_element_type=jnp.float32,
    )


def conv_back_kernel(padded, gradient):
    return lax.conv_general_dilated(
        padded,
        gradient,
        (1, 1, 1),
        "VALID",
        dimension_numbers=("DHWNC", "DHWOI", "DHWNC"),
        preferred_element_type=jnp.float32,
    )


def pooling(values):
    extent_x, extent_y, extent_z, channels, samples = values.shape
    return values.reshape(
        extent_x // 2, 2, extent_y // 2, 2, extent_z // 2, 2, channels, samples
    ).mean(axis=(1, 3, 5))


def spread(values):
    extent_x, extent_y, extent_z, channels, samples = values.shape
    widened = jnp.broadcast_to(
        values[:, None, :, None, :, None],
        (extent_x, 2, extent_y, 2, extent_z, 2, channels, samples),
    )
    return widened.reshape(2 * extent_x, 2 * extent_y, 2 * extent_z, channels, samples)


def fold_faces(inner, from_below, from_above, axis_dim):
    length = inner.shape[axis_dim]
    first = lax.slice_in_dim(inner, 0, 1, axis=axis_dim) + from_below
    middle = lax.slice_in_dim(inner, 1, length - 1, axis=axis_dim)
    last = lax.slice_in_dim(inner, length - 1, length, axis=axis_dim) + from_above
    return jnp.concatenate([first, middle, last], axis=axis_dim)


def body(volume, conv_kernel, dense_one, dense_two, dense_three, targets):
    padded = with_halo(volume, (("gx", 0), ("gy", 1), ("gz", 2)), 1)
    conv_out = conv_forward(padded, conv_kernel)
    pooled = pooling(smooth_leaky(conv_out)).astype(jnp.bfloat16)
    half_x, half_y, half_z, channels, samples = pooled.shape
    groups_y = lax.axis_size("gy")
    groups_z = lax.axis_size("gz")
    per_group = channels // (groups_y * groups_z)
    arrived = lax.all_to_all(pooled[None], ("gy", "gz"), split_axis=4, concat_axis=0, tiled=True)
    arrived = arrived.reshape(groups_y, groups_z, half_x, half_y, half_z, per_group, samples)
    weights_local = dense_one.reshape(
        half_x, groups_y, half_y, groups_z, half_z, per_group, dense_one.shape[4]
    )
    partial_one = jnp.einsum(
        "uvxyzcb,xuyvzch->hb", arrived, weights_local, preferred_element_type=jnp.float32
    )
    pre_one = lax.psum(partial_one, ("gx", "gy", "gz"))
    hidden_one = smooth_leaky(pre_one)
    pre_two = jnp.dot(dense_two.T, hidden_one, precision=lax.Precision.HIGHEST)
    hidden_two = smooth_leaky(pre_two)
    prediction = jnp.dot(dense_three.T, hidden_two, precision=lax.Precision.HIGHEST)
    error_grad = loss_scale * (prediction - targets)
    grad_pre_two = jnp.dot(
        dense_three, error_grad, precision=lax.Precision.HIGHEST
    ) * leaky_derivative(pre_two)
    grad_pre_one = (
        jnp.dot(dense_two, grad_pre_two, precision=lax.Precision.HIGHEST)
        * leaky_derivative(pre_one)
    ).astype(jnp.bfloat16)
    grad_local = jnp.einsum(
        "uvxyzcb,hb->xuyvzch", arrived, grad_pre_one, preferred_element_type=jnp.float32
    )
    grad_dense_one = (grad_local / samples).astype(jnp.bfloat16).reshape(dense_one.shape)
    grad_arrived = jnp.einsum(
        "xuyvzch,hb->uvxyzcb", weights_local, grad_pre_one, preferred_element_type=jnp.float32
    ).astype(jnp.bfloat16)
    outgoing = grad_arrived.reshape(groups_y * groups_z, half_x, half_y, half_z, per_group, samples)
    returned = lax.all_to_all(outgoing, ("gy", "gz"), split_axis=0, concat_axis=4, tiled=True)
    grad_pooled = returned.reshape(half_x, half_y, half_z, channels, samples)
    grad_out = (spread(grad_pooled.astype(jnp.float32)) / 8.0 * leaky_derivative(conv_out)).astype(
        jnp.bfloat16
    )
    widened = jnp.pad(grad_out, ((2, 2), (2, 2), (2, 2), (0, 0), (0, 0)))
    whole = conv_back_input(widened, conv_kernel)
    below_x = from_behind(whole[-1:].astype(jnp.bfloat16), "gx", 1).astype(jnp.float32)
    above_x = from_behind(whole[:1].astype(jnp.bfloat16), "gx", -1).astype(jnp.float32)
    folded = fold_faces(whole[1:-1], below_x, above_x, 0)
    below_y = from_behind(shortened(folded[:, -1:]), "gy", 1)
    above_y = from_behind(shortened(folded[:, :1]), "gy", -1)
    folded = fold_faces(folded[:, 1:-1], below_y, above_y, 1)
    below_z = from_behind(shortened(folded[:, :, -1:]), "gz", 1)
    above_z = from_behind(shortened(folded[:, :, :1]), "gz", -1)
    folded = fold_faces(folded[:, :, 1:-1], below_z, above_z, 2)
    grad_volume = folded.astype(jnp.bfloat16)
    kernel_local = conv_back_kernel(padded, grad_out)
    grad_conv = lax.psum(kernel_local, ("gx", "gy", "gz")) / samples
    return (prediction, grad_dense_one, grad_conv, grad_volume)


def solution(mesh):
    return jax.shard_map(
        body,
        mesh=mesh,
        in_specs=(
            P("gx", "gy", "gz", None, None),
            P(),
            P("gx", None, None, ("gy", "gz"), None),
            P(),
            P(),
            P(),
        ),
        out_specs=(
            P(),
            P("gx", None, None, ("gy", "gz"), None),
            P(),
            P("gx", "gy", "gz", None, None),
        ),
        check_vma=False,
    )
```

profile of v0, /device:TPU:1, one launch (start us, length us, event | category | flops | bytes accessed | tf_op | source)
XLA Modules:
  0.0 538.4 jit_solution(12310446413016146924)
XLA Ops:
  8.4 4.0 collective-permute-start
  13.8 3.7 collective-permute-done
  21.4 7.2 %collective-permute-start.2 = (bf16[10,1,4,32,128]{4,3,2,1,0:T(8,128)(2,1)S(1)}, bf16[10,1,4,32,128]{4,3,2,1,0:T(8,128)(2,1)S(1)}, u32[]{:S(2)}, u32[]{:S(2)}) collective-permute-start(bf16[10,1,4,32,128]{4,3,2,1,0:T(8,128)(2,1)S(1)} %get-tuple-element.18), channel_id=1, source_target_pairs={{0,8},{8,16},{16,24},{1,9},{9,17},{17,25},{2,10},{10,18},{18,26},{... | collective-permute-start | bytes 983048 | tf_op jit(solution)/shard_map/ppermute | solution.py:17
  32.6 23.5 %collective-permute-done.3 = bf16[10,1,4,32,128]{4,3,2,1,0:T(8,128)(2,1)S(1)} collective-permute-done((bf16[10,1,4,32,128]{4,3,2,1,0:T(8,128)(2,1)S(1)}, bf16[10,1,4,32,128]{4,3,2,1,0:T(8,128)(2,1)S(1)}, u32[]{:S(2)}, u32[]{:S(2)}) %collective-permute-start.3) | collective-permute-done | bytes 327712 | tf_op jit(solution)/shard_map/ppermute | solution.py:18
  58.9 7.9 %collective-permute-done.4 = bf16[10,10,1,32,128]{4,3,2,1,0:T(8,128)(2,1)S(1)} collective-permute-done((bf16[10,10,1,32,128]{4,3,2,1,0:T(8,128)(2,1)S(1)}, bf16[10,10,1,32,128]{4,3,2,1,0:T(8,128)(2,1)S(1)}, u32[]{:S(2)}, u32[]{:S(2)}) %collective-permute-start.4) | collective-permute-done | bytes 819232 | tf_op jit(solution)/shard_map/ppermute | solution.py:17
  66.8 3.9 collective-permute-done.5
  70.7 18.1 %fusion.2 = (f32[8,8,4,64,128]{4,3,2,1,0:T(8,128)}, f32[8,8,4,64,128]{4,3,2,1,0:T(8,128)}) fusion(bf16[3,3,3,32,64]{4,3,2,1,0:T(8,128)(2,1)S(1)} %copy-done.12, bf16[10,10,1,32,128]{4,3,2,1,0:T(8,128)(2,1)S(1)} %collective-permute-done.5, bf16[10,1,4,32,128]{4,3,2,1,0:T(8,128)(2,1)S(1)} %collective-permute-done.3, ...), kind=kOutput, calls=%fused_computation.4 | convolution fusion | flops 3652583424 | bytes 21803008 | tf_op jit(solution)/shard_map/conv_general_dilated | solution.py:42
  88.8 4.4 reduce_sum.9
  93.9 13.4 %all_to_all.24 = bf16[1,4,4,2,64,128]{5,3,2,1,0,4:T(2,128)(2,1)S(1)} all-to-all(bf16[1,4,4,2,64,128]{5,3,2,1,0,4:T(2,128)(2,1)S(1)} %copy.45), channel_id=1, replica_groups=mesh['gx'=4,'gy'=4,'gz'=8] {'gy','gz'}, dimensions={4} | all-to-all | bytes 1048576 | tf_op jit(solution)/shard_map/all_to_all | solution.py:107
  107.6 13.7 %fusion.7 = f32[2048,128]{0,1:T(8,128)} fusion(bf16[4,4,4,8,2,2,2048]{6,5,4,3,2,1,0:T(2,128)(2,1)} %bitcast.72, bf16[32,1,4,4,2,2,128]{6,5,0,4,3,2,1:T(2,128)(2,1)S(1)} %bitcast.70), kind=kOutput, calls=%fused_computation.14 | convolution fusion | flops 1073741824 | bytes 9961472 | tf_op jit(solution)/shard_map/uvxyzcb,xuyvzch->hb/dot_general | solution.py:112
  121.6 145.5 %all-reduce.3.cloned.1.call-done = f32[2048,128]{0,1:T(8,128)} async-done(((f32[2048,128]{0,1:T(8,128)}), f32[2048,128]{0,1:T(8,128)}) %all-reduce.3.cloned.1.call-update) | async-done | bytes 1048592 | tf_op jit(solution)/shard_map/psum | solution.py:115
  270.7 3.5 fusion.12
  274.3 8.6 %fusion.16 = bf16[4,8,4,4,2,2,128]{6,1,5,4,3,0,2:T(8,128)(2,1)S(1)} fusion(bf16[2048,128,1,1,1,1,1]{0,1,6,5,4,3,2:T(8,128)(2,1)S(1)} %fusion.12, bf16[4,4,4,8,2,2,2048]{6,5,4,3,2,1,0:T(2,128)(2,1)} %bitcast.73), kind=kOutput, calls=%fused_computation.21 | convolution fusion | flops 1074003968 | bytes 9437184 | tf_op jit(solution)/shard_map/xuyvzch,hb->uvxyzcb/dot_general | solution.py:132
  283.6 17.6 %all_to_all.25 = bf16[32,4,4,2,2,128]{5,4,3,2,1,0:T(2,128)(2,1)S(1)} all-to-all(bf16[32,4,4,2,2,128]{5,4,3,2,1,0:T(2,128)(2,1)S(1)} %copy.56), channel_id=1, replica_groups=mesh['gx'=4,'gy'=4,'gz'=8] {'gy','gz'}, dimensions={0} | all-to-all | bytes 1048576 | tf_op jit(solution)/shard_map/all_to_all | solution.py:136
  307.3 29.9 %fusion.70 = (bf16[10,10,6,32,128]{4,3,2,1,0:T(8,128)(2,1)S(1)}, f32[10,10,6,32,128]{4,3,2,1,0:T(8,128)S(1)}) fusion(bf16[8,8,4,64,128]{4,3,2,1,0:T(8,128)(2,1)S(1)} %multiply_convert_fusion.1, bf16[3,3,3,32,64]{4,3,2,1,0:T(8,128)(2,1)S(1)} %copy-done.13), kind=kOutput, calls=%fused_computation.92 | convolution fusion | flops 3626336256 | bytes 19050496 | tf_op jit(solution)/shard_map/conv_general_dilated | solution.py:54
  341.8 7.6 %collective-permute-done.6 = bf16[1,10,6,32,128]{4,3,2,1,0:T(8,128)(2,1)S(1)} collective-permute-done((bf16[1,10,6,32,128]{4,3,2,1,0:T(8,128)(2,1)S(1)}, bf16[1,10,6,32,128]{4,3,2,1,0:T(8,128)(2,1)S(1)}, u32[]{:S(2)}, u32[]{:S(2)}) %collective-permute-start.6) | collective-permute-done | bytes 491552 | tf_op jit(solution)/shard_map/ppermute | solution.py:26
  349.4 3.9 collective-permute-done.7
  354.4 4.0 collective-permute-start.8
  360.6 15.5 %fusion.61 = f32[3,3,3,32,64]{4,3,2,1,0:T(8,128)} fusion(bf16[8,8,4,64,128]{4,3,2,1,0:T(8,128)(2,1)S(1)} %multiply_convert_fusion.1, bf16[10,10,1,32,128]{4,3,2,1,0:T(8,128)(2,1)S(1)} %copy-done.17, bf16[10,1,4,32,128]{4,3,2,1,0:T(8,128)(2,1)S(1)} %copy-done.11, bf16[10,8,4,32,128]{4,3,2,1,0:T(8,128)(2,1)S(1)} %copy-done.7, ...), kind=kOutput, calls=%fused_computation.83 | convolution fusion | flops 3633709056 | bytes 9330688 | tf_op jit(solution)/shard_map/conv_general_dilated | solution.py:65
  376.1 3.5 pad_maximum_fusion
  383.9 3.0 collective-permute-start.10
  390.7 9.4 %copy.52 = bf16[4,4,4,8,2,2,2048]{6,5,4,3,2,1,0:T(2,128)(2,1)} copy(bf16[4,4,4,8,2,2,2048]{6,3,5,4,2,0,1:T(8,128)(2,1)S(1)} %fusion) | data formatting | bytes 16777216 | tf_op jit(solution)/shard_map/convert_element_type | solution.py:131
  400.0 122.7 %all-reduce.5.cloned.1.call-done = f32[3,3,3,32,64]{4,3,2,1,0:T(8,128)} async-done(((f32[3,3,3,32,64]{4,3,2,1,0:T(8,128)}), f32[3,3,3,32,64]{4,3,2,1,0:T(8,128)}) %all-reduce.5.cloned.1.call-update) | async-done | bytes 221200 | tf_op jit(solution)/shard_map/psum | solution.py:154
  524.6 3.4 pad_maximum_fusion.1
  (102 shorter events, 45.7 us)
Async XLA Ops:
  7.2 259.9 %copy-start = (f32[2048,256]{1,0:T(8,128)S(1)}, f32[2048,256]{1,0:T(8,128)}, u32[]{:S(2)}) copy-start(f32[2048,256]{1,0:T(8,128)} %param.9) | copy-start | bytes 6291460
  7.2 259.9 %all-reduce.3.cloned.1.call-start = ((), (), s32[]{:S(2)}) async-start(), calls=%async_computation.2 | async-start | bytes 2097152 | tf_op jit(solution)/shard_map/psum | solution.py:115
  8.4 9.0 %collective-permute-start = (bf16[1,8,4,32,128]{4,3,2,1,0:T(8,128)(2,1)S(1)}, bf16[1,8,4,32,128]{4,3,2,1,0:T(8,128)(2,1)S(1)}, u32[]{:S(2)}, u32[]{:S(2)}) collective-permute-start(bf16[1,8,4,32,128]{4,3,2,1,0:T(8,128)(2,1)S(1)} %get-tuple-element.21), channel_id=1, source_target_pairs={{0,32},{32,64},{64,96},{1,33},{33,65},{65,97},{2,34},{34,66},{66,9... | collective-permute-start | bytes 786440 | tf_op jit(solution)/shard_map/ppermute | solution.py:17
  12.5 8.8 %collective-permute-start.1 = (bf16[1,8,4,32,128]{4,3,2,1,0:T(8,128)(2,1)S(1)}, bf16[1,8,4,32,128]{4,3,2,1,0:T(8,128)(2,1)S(1)}, u32[]{:S(2)}, u32[]{:S(2)}) collective-permute-start(bf16[1,8,4,32,128]{4,3,2,1,0:T(8,128)(2,1)S(1)} %get-tuple-element.20), channel_id=1, source_target_pairs={{32,0},{64,32},{96,64},{33,1},{65,33},{97,65},{34,2},{66,34},{98,6... | collective-permute-start | bytes 786440 | tf_op jit(solution)/shard_map/ppermute | solution.py:18
  17.5 53.2 %copy-start.12 = (bf16[3,3,3,32,64]{4,3,2,1,0:T(8,128)(2,1)S(1)}, bf16[3,3,3,32,64]{4,3,2,1,0:T(8,128)(2,1)}, u32[]{:S(2)}) copy-start(bf16[3,3,3,32,64]{4,3,2,1,0:T(8,128)(2,1)} %param.7) | copy-start | bytes 331780
  21.3 67.4 %copy-start.6 = (bf16[10,8,4,32,128]{4,3,2,1,0:T(8,128)(2,1)}, bf16[10,8,4,32,128]{4,3,2,1,0:T(8,128)(2,1)S(1)}, u32[]{:S(2)}) copy-start(bf16[10,8,4,32,128]{4,3,2,1,0:T(8,128)(2,1)S(1)} %constant_dynamic-update-slice_fusion) | copy-start | bytes 7864324
  21.4 11.2 %collective-permute-start.2 = (bf16[10,1,4,32,128]{4,3,2,1,0:T(8,128)(2,1)S(1)}, bf16[10,1,4,32,128]{4,3,2,1,0:T(8,128)(2,1)S(1)}, u32[]{:S(2)}, u32[]{:S(2)}) collective-permute-start(bf16[10,1,4,32,128]{4,3,2,1,0:T(8,128)(2,1)S(1)} %get-tuple-element.18), channel_id=1, source_target_pairs={{0,8},{8,16},{16,24},{1,9},{9,17},{17,25},{2,10},{10,18},{18,26},{... | collective-permute-start | bytes 983048 | tf_op jit(solution)/shard_map/ppermute | solution.py:17
  28.6 27.5 %collective-permute-start.3 = (bf16[10,1,4,32,128]{4,3,2,1,0:T(8,128)(2,1)S(1)}, bf16[10,1,4,32,128]{4,3,2,1,0:T(8,128)(2,1)S(1)}, u32[]{:S(2)}, u32[]{:S(2)}) collective-permute-start(bf16[10,1,4,32,128]{4,3,2,1,0:T(8,128)(2,1)S(1)} %get-tuple-element.19), channel_id=1, source_target_pairs={{8,0},{16,8},{24,16},{9,1},{17,9},{25,17},{10,2},{18,10},{26,18},{... | collective-permute-start | bytes 983048 | tf_op jit(solution)/shard_map/ppermute | solution.py:18
  32.6 56.2 %copy-start.8 = (bf16[10,1,4,32,128]{4,3,2,1,0:T(8,128)(2,1)}, bf16[10,1,4,32,128]{4,3,2,1,0:T(8,128)(2,1)S(1)}, u32[]{:S(2)}) copy-start(bf16[10,1,4,32,128]{4,3,2,1,0:T(8,128)(2,1)S(1)} %collective-permute-done.2) | copy-start | bytes 983044
  56.1 32.7 %copy-start.10 = (bf16[10,1,4,32,128]{4,3,2,1,0:T(8,128)(2,1)}, bf16[10,1,4,32,128]{4,3,2,1,0:T(8,128)(2,1)S(1)}, u32[]{:S(2)}) copy-start(bf16[10,1,4,32,128]{4,3,2,1,0:T(8,128)(2,1)S(1)} %collective-permute-done.3) | copy-start | bytes 983044
  56.3 10.6 %collective-permute-start.4 = (bf16[10,10,1,32,128]{4,3,2,1,0:T(8,128)(2,1)S(1)}, bf16[10,10,1,32,128]{4,3,2,1,0:T(8,128)(2,1)S(1)}, u32[]{:S(2)}, u32[]{:S(2)}) collective-permute-start(bf16[10,10,1,32,128]{4,3,2,1,0:T(8,128)(2,1)S(1)} %get-tuple-element.14), channel_id=1, source_target_pairs={{0,1},{1,2},{2,3},{3,4},{4,5},{5,6},{6,7},{8,9},{9,10},{10,11},{11... | collective-permute-start | bytes 2457608 | tf_op jit(solution)/shard_map/ppermute | solution.py:17
  57.6 13.1 %collective-permute-start.5 = (bf16[10,10,1,32,128]{4,3,2,1,0:T(8,128)(2,1)S(1)}, bf16[10,10,1,32,128]{4,3,2,1,0:T(8,128)(2,1)S(1)}, u32[]{:S(2)}, u32[]{:S(2)}) collective-permute-start(bf16[10,10,1,32,128]{4,3,2,1,0:T(8,128)(2,1)S(1)} %get-tuple-element.15), channel_id=1, source_target_pairs={{1,0},{2,1},{3,2},{4,3},{5,4},{6,5},{7,6},{9,8},{10,9},{11,10},{12... | collective-permute-start | bytes 2457608 | tf_op jit(solution)/shard_map/ppermute | solution.py:18
  66.8 22.0 %copy-start.14 = (bf16[10,10,1,32,128]{4,3,2,1,0:T(8,128)(2,1)}, bf16[10,10,1,32,128]{4,3,2,1,0:T(8,128)(2,1)S(1)}, u32[]{:S(2)}) copy-start(bf16[10,10,1,32,128]{4,3,2,1,0:T(8,128)(2,1)S(1)} %collective-permute-done.4) | copy-start | bytes 2457604
  70.7 18.1 %copy-start.16 = (bf16[10,10,1,32,128]{4,3,2,1,0:T(8,128)(2,1)}, bf16[10,10,1,32,128]{4,3,2,1,0:T(8,128)(2,1)S(1)}, u32[]{:S(2)}) copy-start(bf16[10,10,1,32,128]{4,3,2,1,0:T(8,128)(2,1)S(1)} %collective-permute-done.5) | copy-start | bytes 2457604
  107.5 162.5 %copy-start.18 = (f32[256,4]{0,1:T(4,128)S(1)}, f32[256,4]{0,1:T(4,128)}, u32[]{:S(2)}) copy-start(f32[256,4]{0,1:T(4,128)} %param.10) | copy-start | bytes 12292
  107.6 162.8 %copy-start.19 = (f32[4,128]{1,0:T(4,128)S(1)}, f32[4,128]{1,0:T(4,128)}, u32[]{:S(2)}) copy-start(f32[4,128]{1,0:T(4,128)} %param.11) | copy-start | bytes 6148
  121.3 401.4 %all-reduce.5.cloned.1.call-start = ((), (), s32[]{:S(2)}) async-start(), calls=%async_computation.3 | async-start | bytes 884736 | tf_op jit(solution)/shard_map/psum | solution.py:154
  283.0 20.3 %slice-start.1 = ((s8[8388608]{0:T(1024)(128)(4,1)}), s8[4194304]{0:T(1024)(128)(4,1)S(1)}, s32[]{:S(2)}) async-start(s8[8388608]{0:T(1024)(128)(4,1)} %bitcast.65), calls=%async_computation.5 | async-start | bytes 8388608
  337.3 12.2 %collective-permute-start.6 = (bf16[1,10,6,32,128]{4,3,2,1,0:T(8,128)(2,1)S(1)}, bf16[1,10,6,32,128]{4,3,2,1,0:T(8,128)(2,1)S(1)}, u32[]{:S(2)}, u32[]{:S(2)}) collective-permute-start(bf16[1,10,6,32,128]{4,3,2,1,0:T(8,128)(2,1)S(1)} %get-tuple-element.10), channel_id=1, source_target_pairs={{0,32},{32,64},{64,96},{1,33},{33,65},{65,97},{2,34},{34,66},{66,9... | collective-permute-start | bytes 1474568 | tf_op jit(solution)/shard_map/ppermute | solution.py:26
  339.3 14.0 %collective-permute-start.7 = (bf16[1,10,6,32,128]{4,3,2,1,0:T(8,128)(2,1)S(1)}, bf16[1,10,6,32,128]{4,3,2,1,0:T(8,128)(2,1)S(1)}, u32[]{:S(2)}, u32[]{:S(2)}) collective-permute-start(bf16[1,10,6,32,128]{4,3,2,1,0:T(8,128)(2,1)S(1)} %get-tuple-element.11), channel_id=1, source_target_pairs={{32,0},{64,32},{96,64},{33,1},{65,33},{97,65},{34,2},{66,34},{98,6... | collective-permute-start | bytes 1474568 | tf_op jit(solution)/shard_map/ppermute | solution.py:26
  354.4 25.7 %collective-permute-start.8 = (bf16[8,1,6,32,128]{4,3,2,1,0:T(8,128)(2,1)S(1)}, bf16[8,1,6,32,128]{4,3,2,1,0:T(8,128)(2,1)}, u32[]{:S(2)}, u32[]{:S(2)}) collective-permute-start(bf16[8,1,6,32,128]{4,3,2,1,0:T(8,128)(2,1)S(1)} %get-tuple-element.12), channel_id=1, source_target_pairs={{0,8},{8,16},{16,24},{1,9},{9,17},{17,25},{2,10},{10,18},{18,26},{... | collective-permute-start | bytes 1179656 | tf_op jit(solution)/shard_map/ppermute | solution.py:26
  358.4 21.7 %collective-permute-start.9 = (bf16[8,1,6,32,128]{4,3,2,1,0:T(8,128)(2,1)S(1)}, bf16[8,1,6,32,128]{4,3,2,1,0:T(8,128)(2,1)}, u32[]{:S(2)}, u32[]{:S(2)}) collective-permute-start(bf16[8,1,6,32,128]{4,3,2,1,0:T(8,128)(2,1)S(1)} %get-tuple-element.13), channel_id=1, source_target_pairs={{8,0},{16,8},{24,16},{9,1},{17,9},{25,17},{10,2},{18,10},{26,18},{... | collective-permute-start | bytes 1179656 | tf_op jit(solution)/shard_map/ppermute | solution.py:26
  383.9 144.2 %collective-permute-start.10 = (bf16[8,8,1,32,128]{4,3,2,1,0:T(8,128)(2,1)}, bf16[8,8,1,32,128]{4,3,2,1,0:T(8,128)(2,1)}, u32[]{:S(2)}, u32[]{:S(2)}) collective-permute-start(bf16[8,8,1,32,128]{4,3,2,1,0:T(8,128)(2,1)} %get-tuple-element.16), channel_id=1, source_target_pairs={{0,1},{1,2},{2,3},{3,4},{4,5},{5,6},{6,7},{8,9},{9,10},{10,11},{11... | collective-permute-start | bytes 1572872 | tf_op jit(solution)/shard_map/ppermute | solution.py:26
  386.8 141.2 %collective-permute-start.11 = (bf16[8,8,1,32,128]{4,3,2,1,0:T(8,128)(2,1)}, bf16[8,8,1,32,128]{4,3,2,1,0:T(8,128)(2,1)}, u32[]{:S(2)}, u32[]{:S(2)}) collective-permute-start(bf16[8,8,1,32,128]{4,3,2,1,0:T(8,128)(2,1)} %get-tuple-element.17), channel_id=1, source_target_pairs={{1,0},{2,1},{3,2},{4,3},{5,4},{6,5},{7,6},{9,8},{10,9},{11,10},{12... | collective-permute-start | bytes 1572872 | tf_op jit(solution)/shard_map/ppermute | solution.py:26
  (16 other events, 100.1 us)
Sparse Core Ops, SparseCore 0:
  121.4 145.5 all-reduce.2
  376.2 146.5 all-reduce.4
where the time goes:
time: 547 us; the launch traced here: 538 us
  waiting for transfers between devices  322 us (59%)
  matrix products  95.2 us (17%)
  starting transfers between devices  31.3 us (6%)
  blocking collectives  31 us (6%)
  other arithmetic  23.4 us (4%)
  local copies, waits for them, and re-layouts  20.5 us (4%)
  between operations  14.9 us (3%)
    psum x1, waiting for transfers between devices, body(): pre_one = lax.psum(partial_one, ('gx', 'gy', 'gz'))  145 us
    psum x1, waiting for transfers between devices, body(): grad_conv = lax.psum(kernel_local, ('gx', 'gy', 'gz')) / samples  123 us
    conv_general_dilated x1, matrix products, conv_back_input(): lax.conv_general_dilated(padded_grad, flipped, (1, 1, 1), 'VALID', dimens...  29.9 us
    ppermute x3, waiting for transfers between devices, with_halo(): after = lax.ppermute(initial, axis, down)  28.7 us
    conv_general_dilated x1, matrix products, conv_forward(): lax.conv_general_dilated(padded, kernel, (1, 1, 1), 'VALID', dimension_nu...  18.1 us
    all_to_all x1, blocking collectives, body(): lax.all_to_all(outgoing, ('gy', 'gz'), split_axis=0, concat_axis=4, tiled...  17.6 us
    conv_general_dilated x1, matrix products, conv_back_kernel(): lax.conv_general_dilated(padded, gradient, (1, 1, 1), 'VALID', dimension_...  15.5 us
    ppermute x6, starting transfers between devices, from_behind(): return lax.ppermute(block, axis, route)  13.9 us
  transfers between devices with their start and end apart: 14, of which 10 were waited for; matrix products, arithmetic and copies ran while one was open for 8% of the time, Pallas kernels for 0%

commit v1 on v0

--- a/solution.py
+++ b/solution.py
@@ -112,7 +112,7 @@
     partial_one = jnp.einsum(
         "uvxyzcb,xuyvzch->hb", arrived, weights_local, preferred_element_type=jnp.float32
     )
-    pre_one = lax.psum(partial_one, ("gx", "gy", "gz"))
+    pre_one = lax.psum(lax.psum(partial_one, ("gy", "gz")), "gx")
     hidden_one = smooth_leaky(pre_one)
     pre_two = jnp.dot(dense_two.T, hidden_one, precision=lax.Precision.HIGHEST)
     hidden_two = smooth_leaky(pre_two)

time: 547 us -> 553 us (1.011)
    psum x1 -> x2, waiting for transfers between devices: 145 us -> 149 us  [body(): pre_one = lax.psum(lax.psum(partial_one, ('gy', 'gz')), 'gx')]
  transfers between devices with their start and end apart: 14 -> 15, of which waited for: 10 -> 11; matrix products, arithmetic and copies ran while one was open for 8% -> 8% of each run, Pallas kernels for 0% -> 0%
where the time goes in v1:
time: 553 us; the launch traced here: 545 us
  waiting for transfers between devices  325 us (59%)
  matrix products  95.2 us (17%)
  blocking collectives  34.4 us (6%)
  starting transfers between devices  31.7 us (6%)
  other arithmetic  23.4 us (4%)
  local copies, waits for them, and re-layouts  20.5 us (4%)
  between operations  14.6 us (3%)
    psum x2, waiting for transfers between devices, body(): pre_one = lax.psum(lax.psum(partial_one, ('gy', 'gz')), 'gx')  149 us
    psum x1, waiting for transfers between devices, body(): grad_conv = lax.psum(kernel_local, ('gx', 'gy', 'gz')) / samples  122 us
    conv_general_dilated x1, matrix products, conv_back_input(): lax.conv_general_dilated(padded_grad, flipped, (1, 1, 1), 'VALID', dimens...  29.9 us
    ppermute x3, waiting for transfers between devices, with_halo(): after = lax.ppermute(initial, axis, down)  28.7 us
    all_to_all x1, blocking collectives, body(): lax.all_to_all(outgoing, ('gy', 'gz'), split_axis=0, concat_axis=4, tiled...  20.9 us
    conv_general_dilated x1, matrix products, conv_forward(): lax.conv_general_dilated(padded, kernel, (1, 1, 1), 'VALID', dimension_nu...  18.1 us
    conv_general_dilated x1, matrix products, conv_back_kernel(): lax.conv_general_dilated(padded, gradient, (1, 1, 1), 'VALID', dimension_...  15.5 us
    ppermute x6, starting transfers between devices, from_behind(): return lax.ppermute(block, axis, route)  14.3 us
  transfers between devices with their start and end apart: 15, of which 11 were waited for; matrix products, arithmetic and copies ran while one was open for 8% of the time, Pallas kernels for 0%

profile of v1, /device:TPU:1, one launch (start us, length us, event | category | flops | bytes accessed | tf_op | source)
XLA Modules:
  0.0 545.1 jit_solution(5601406323933363507)
XLA Ops:
  8.4 4.0 collective-permute-start
  13.8 3.7 collective-permute-done
  21.4 7.2 %collective-permute-start.2 = (bf16[10,1,4,32,128]{4,3,2,1,0:T(8,128)(2,1)S(1)}, bf16[10,1,4,32,128]{4,3,2,1,0:T(8,128)(2,1)S(1)}, u32[]{:S(2)}, u32[]{:S(2)}) collective-permute-start(bf16[10,1,4,32,128]{4,3,2,1,0:T(8,128)(2,1)S(1)} %get-tuple-element.18), channel_id=1, source_target_pairs={{0,8},{8,16},{16,24},{1,9},{9,17},{17,25},{2,10},{10,18},{18,26},{... | collective-permute-start | bytes 983048 | tf_op jit(solution)/shard_map/ppermute | solution.py:17
  32.6 23.5 %collective-permute-done.3 = bf16[10,1,4,32,128]{4,3,2,1,0:T(8,128)(2,1)S(1)} collective-permute-done((bf16[10,1,4,32,128]{4,3,2,1,0:T(8,128)(2,1)S(1)}, bf16[10,1,4,32,128]{4,3,2,1,0:T(8,128)(2,1)S(1)}, u32[]{:S(2)}, u32[]{:S(2)}) %collective-permute-start.3) | collective-permute-done | bytes 327712 | tf_op jit(solution)/shard_map/ppermute | solution.py:18
  58.9 7.9 %collective-permute-done.4 = bf16[10,10,1,32,128]{4,3,2,1,0:T(8,128)(2,1)S(1)} collective-permute-done((bf16[10,10,1,32,128]{4,3,2,1,0:T(8,128)(2,1)S(1)}, bf16[10,10,1,32,128]{4,3,2,1,0:T(8,128)(2,1)S(1)}, u32[]{:S(2)}, u32[]{:S(2)}) %collective-permute-start.4) | collective-permute-done | bytes 819232 | tf_op jit(solution)/shard_map/ppermute | solution.py:17
  66.8 3.9 collective-permute-done.5
  70.7 18.1 %fusion.2 = (f32[8,8,4,64,128]{4,3,2,1,0:T(8,128)}, f32[8,8,4,64,128]{4,3,2,1,0:T(8,128)}) fusion(bf16[3,3,3,32,64]{4,3,2,1,0:T(8,128)(2,1)S(1)} %copy-done.12, bf16[10,10,1,32,128]{4,3,2,1,0:T(8,128)(2,1)S(1)} %collective-permute-done.5, bf16[10,1,4,32,128]{4,3,2,1,0:T(8,128)(2,1)S(1)} %collective-permute-done.3, ...), kind=kOutput, calls=%fused_computation.4 | convolution fusion | flops 3652583424 | bytes 21803008 | tf_op jit(solution)/shard_map/conv_general_dilated | solution.py:42
  88.8 4.4 reduce_sum.9
  93.9 13.4 %all_to_all.24 = bf16[1,4,4,2,64,128]{5,3,2,1,0,4:T(2,128)(2,1)S(1)} all-to-all(bf16[1,4,4,2,64,128]{5,3,2,1,0,4:T(2,128)(2,1)S(1)} %copy.45), channel_id=1, replica_groups=mesh['gx'=4,'gy'=4,'gz'=8] {'gy','gz'}, dimensions={4} | all-to-all | bytes 1048576 | tf_op jit(solution)/shard_map/all_to_all | solution.py:107
  107.5 13.7 %fusion.7 = f32[2048,128]{0,1:T(8,128)} fusion(bf16[4,4,4,8,2,2,2048]{6,5,4,3,2,1,0:T(2,128)(2,1)} %bitcast.72, bf16[32,1,4,4,2,2,128]{6,5,0,4,3,2,1:T(2,128)(2,1)S(1)} %bitcast.70), kind=kOutput, calls=%fused_computation.14 | convolution fusion | flops 1073741824 | bytes 9961472 | tf_op jit(solution)/shard_map/uvxyzcb,xuyvzch->hb/dot_general | solution.py:112
  121.4 103.0 %all-reduce.4.cloned.1.call-done = f32[2048,128]{0,1:T(8,128)} async-done(((f32[2048,128]{0,1:T(8,128)}), f32[2048,128]{0,1:T(8,128)}) %all-reduce.4.cloned.1.call-update) | async-done | bytes 1048592 | tf_op jit(solution)/shard_map/psum | solution.py:115
  224.6 45.9 %all-reduce.6.cloned.1.call-done = f32[2048,128]{0,1:T(8,128)} async-done(((f32[2048,128]{0,1:T(8,128)}), f32[2048,128]{0,1:T(8,128)}) %all-reduce.6.cloned.1.call-update) | async-done | bytes 1048592 | tf_op jit(solution)/shard_map/psum | solution.py:115
  274.1 3.5 fusion.12
  277.7 8.6 %fusion.16 = bf16[4,8,4,4,2,2,128]{6,1,5,4,3,0,2:T(8,128)(2,1)S(1)} fusion(bf16[2048,128,1,1,1,1,1]{0,1,6,5,4,3,2:T(8,128)(2,1)S(1)} %fusion.12, bf16[4,4,4,8,2,2,2048]{6,5,4,3,2,1,0:T(2,128)(2,1)} %bitcast.73), kind=kOutput, calls=%fused_computation.21 | convolution fusion | flops 1074003968 | bytes 9437184 | tf_op jit(solution)/shard_map/xuyvzch,hb->uvxyzcb/dot_general | solution.py:132
  287.0 20.9 %all_to_all.25 = bf16[32,4,4,2,2,128]{5,4,3,2,1,0:T(2,128)(2,1)S(1)} all-to-all(bf16[32,4,4,2,2,128]{5,4,3,2,1,0:T(2,128)(2,1)S(1)} %copy.56), channel_id=1, replica_groups=mesh['gx'=4,'gy'=4,'gz'=8] {'gy','gz'}, dimensions={0} | all-to-all | bytes 1048576 | tf_op jit(solution)/shard_map/all_to_all | solution.py:136
  314.1 29.9 %fusion.70 = (bf16[10,10,6,32,128]{4,3,2,1,0:T(8,128)(2,1)S(1)}, f32[10,10,6,32,128]{4,3,2,1,0:T(8,128)S(1)}) fusion(bf16[8,8,4,64,128]{4,3,2,1,0:T(8,128)(2,1)S(1)} %multiply_convert_fusion.1, bf16[3,3,3,32,64]{4,3,2,1,0:T(8,128)(2,1)S(1)} %copy-done.13), kind=kOutput, calls=%fused_computation.92 | convolution fusion | flops 3626336256 | bytes 19050496 | tf_op jit(solution)/shard_map/conv_general_dilated | solution.py:54
  349.1 7.6 %collective-permute-done.6 = bf16[1,10,6,32,128]{4,3,2,1,0:T(8,128)(2,1)S(1)} collective-permute-done((bf16[1,10,6,32,128]{4,3,2,1,0:T(8,128)(2,1)S(1)}, bf16[1,10,6,32,128]{4,3,2,1,0:T(8,128)(2,1)S(1)}, u32[]{:S(2)}, u32[]{:S(2)}) %collective-permute-start.6) | collective-permute-done | bytes 491552 | tf_op jit(solution)/shard_map/ppermute | solution.py:26
  356.7 4.0 collective-permute-done.7
  361.8 3.9 collective-permute-start.8
  367.8 15.5 %fusion.61 = f32[3,3,3,32,64]{4,3,2,1,0:T(8,128)} fusion(bf16[8,8,4,64,128]{4,3,2,1,0:T(8,128)(2,1)S(1)} %multiply_convert_fusion.1, bf16[10,10,1,32,128]{4,3,2,1,0:T(8,128)(2,1)S(1)} %copy-done.17, bf16[10,1,4,32,128]{4,3,2,1,0:T(8,128)(2,1)S(1)} %copy-done.11, bf16[10,8,4,32,128]{4,3,2,1,0:T(8,128)(2,1)S(1)} %copy-done.7, ...), kind=kOutput, calls=%fused_computation.83 | convolution fusion | flops 3633709056 | bytes 9330688 | tf_op jit(solution)/shard_map/conv_general_dilated | solution.py:65
  383.3 3.5 pad_maximum_fusion
  398.0 9.4 %copy.52 = bf16[4,4,4,8,2,2,2048]{6,5,4,3,2,1,0:T(2,128)(2,1)} copy(bf16[4,4,4,8,2,2,2048]{6,3,5,4,2,0,1:T(8,128)(2,1)S(1)} %fusion) | data formatting | bytes 16777216 | tf_op jit(solution)/shard_map/convert_element_type | solution.py:131
  407.3 122.5 %all-reduce.8.cloned.1.call-done = f32[3,3,3,32,64]{4,3,2,1,0:T(8,128)} async-done(((f32[3,3,3,32,64]{4,3,2,1,0:T(8,128)}), f32[3,3,3,32,64]{4,3,2,1,0:T(8,128)}) %all-reduce.8.cloned.1.call-update) | async-done | bytes 221200 | tf_op jit(solution)/shard_map/psum | solution.py:154
  531.6 3.4 pad_maximum_fusion.1
  (105 shorter events, 49.2 us)
Async XLA Ops:
  7.2 263.3 %copy-start = (f32[2048,256]{1,0:T(8,128)S(1)}, f32[2048,256]{1,0:T(8,128)}, u32[]{:S(2)}) copy-start(f32[2048,256]{1,0:T(8,128)} %param.9) | copy-start | bytes 6291460
  7.2 217.1 %all-reduce.4.cloned.1.call-start = ((), (), s32[]{:S(2)}) async-start(), calls=%async_computation.2 | async-start | bytes 2097152 | tf_op jit(solution)/shard_map/psum | solution.py:115
  8.4 9.0 %collective-permute-start = (bf16[1,8,4,32,128]{4,3,2,1,0:T(8,128)(2,1)S(1)}, bf16[1,8,4,32,128]{4,3,2,1,0:T(8,128)(2,1)S(1)}, u32[]{:S(2)}, u32[]{:S(2)}) collective-permute-start(bf16[1,8,4,32,128]{4,3,2,1,0:T(8,128)(2,1)S(1)} %get-tuple-element.21), channel_id=1, source_target_pairs={{0,32},{32,64},{64,96},{1,33},{33,65},{65,97},{2,34},{34,66},{66,9... | collective-permute-start | bytes 786440 | tf_op jit(solution)/shard_map/ppermute | solution.py:17
  12.5 8.8 %collective-permute-start.1 = (bf16[1,8,4,32,128]{4,3,2,1,0:T(8,128)(2,1)S(1)}, bf16[1,8,4,32,128]{4,3,2,1,0:T(8,128)(2,1)S(1)}, u32[]{:S(2)}, u32[]{:S(2)}) collective-permute-start(bf16[1,8,4,32,128]{4,3,2,1,0:T(8,128)(2,1)S(1)} %get-tuple-element.20), channel_id=1, source_target_pairs={{32,0},{64,32},{96,64},{33,1},{65,33},{97,65},{34,2},{66,34},{98,6... | collective-permute-start | bytes 786440 | tf_op jit(solution)/shard_map/ppermute | solution.py:18
  17.5 53.2 %copy-start.12 = (bf16[3,3,3,32,64]{4,3,2,1,0:T(8,128)(2,1)S(1)}, bf16[3,3,3,32,64]{4,3,2,1,0:T(8,128)(2,1)}, u32[]{:S(2)}) copy-start(bf16[3,3,3,32,64]{4,3,2,1,0:T(8,128)(2,1)} %param.7) | copy-start | bytes 331780
  21.3 67.4 %copy-start.6 = (bf16[10,8,4,32,128]{4,3,2,1,0:T(8,128)(2,1)}, bf16[10,8,4,32,128]{4,3,2,1,0:T(8,128)(2,1)S(1)}, u32[]{:S(2)}) copy-start(bf16[10,8,4,32,128]{4,3,2,1,0:T(8,128)(2,1)S(1)} %constant_dynamic-update-slice_fusion) | copy-start | bytes 7864324
  21.4 11.2 %collective-permute-start.2 = (bf16[10,1,4,32,128]{4,3,2,1,0:T(8,128)(2,1)S(1)}, bf16[10,1,4,32,128]{4,3,2,1,0:T(8,128)(2,1)S(1)}, u32[]{:S(2)}, u32[]{:S(2)}) collective-permute-start(bf16[10,1,4,32,128]{4,3,2,1,0:T(8,128)(2,1)S(1)} %get-tuple-element.18), channel_id=1, source_target_pairs={{0,8},{8,16},{16,24},{1,9},{9,17},{17,25},{2,10},{10,18},{18,26},{... | collective-permute-start | bytes 983048 | tf_op jit(solution)/shard_map/ppermute | solution.py:17
  28.6 27.5 %collective-permute-start.3 = (bf16[10,1,4,32,128]{4,3,2,1,0:T(8,128)(2,1)S(1)}, bf16[10,1,4,32,128]{4,3,2,1,0:T(8,128)(2,1)S(1)}, u32[]{:S(2)}, u32[]{:S(2)}) collective-permute-start(bf16[10,1,4,32,128]{4,3,2,1,0:T(8,128)(2,1)S(1)} %get-tuple-element.19), channel_id=1, source_target_pairs={{8,0},{16,8},{24,16},{9,1},{17,9},{25,17},{10,2},{18,10},{26,18},{... | collective-permute-start | bytes 983048 | tf_op jit(solution)/shard_map/ppermute | solution.py:18
  32.6 56.2 %copy-start.8 = (bf16[10,1,4,32,128]{4,3,2,1,0:T(8,128)(2,1)}, bf16[10,1,4,32,128]{4,3,2,1,0:T(8,128)(2,1)S(1)}, u32[]{:S(2)}) copy-start(bf16[10,1,4,32,128]{4,3,2,1,0:T(8,128)(2,1)S(1)} %collective-permute-done.2) | copy-start | bytes 983044
  56.1 32.7 %copy-start.10 = (bf16[10,1,4,32,128]{4,3,2,1,0:T(8,128)(2,1)}, bf16[10,1,4,32,128]{4,3,2,1,0:T(8,128)(2,1)S(1)}, u32[]{:S(2)}) copy-start(bf16[10,1,4,32,128]{4,3,2,1,0:T(8,128)(2,1)S(1)} %collective-permute-done.3) | copy-start | bytes 983044
  56.3 10.6 %collective-permute-start.4 = (bf16[10,10,1,32,128]{4,3,2,1,0:T(8,128)(2,1)S(1)}, bf16[10,10,1,32,128]{4,3,2,1,0:T(8,128)(2,1)S(1)}, u32[]{:S(2)}, u32[]{:S(2)}) collective-permute-start(bf16[10,10,1,32,128]{4,3,2,1,0:T(8,128)(2,1)S(1)} %get-tuple-element.14), channel_id=1, source_target_pairs={{0,1},{1,2},{2,3},{3,4},{4,5},{5,6},{6,7},{8,9},{9,10},{10,11},{11... | collective-permute-start | bytes 2457608 | tf_op jit(solution)/shard_map/ppermute | solution.py:17
  57.6 13.1 %collective-permute-start.5 = (bf16[10,10,1,32,128]{4,3,2,1,0:T(8,128)(2,1)S(1)}, bf16[10,10,1,32,128]{4,3,2,1,0:T(8,128)(2,1)S(1)}, u32[]{:S(2)}, u32[]{:S(2)}) collective-permute-start(bf16[10,10,1,32,128]{4,3,2,1,0:T(8,128)(2,1)S(1)} %get-tuple-element.15), channel_id=1, source_target_pairs={{1,0},{2,1},{3,2},{4,3},{5,4},{6,5},{7,6},{9,8},{10,9},{11,10},{12... | collective-permute-start | bytes 2457608 | tf_op jit(solution)/shard_map/ppermute | solution.py:18
  66.8 22.0 %copy-start.14 = (bf16[10,10,1,32,128]{4,3,2,1,0:T(8,128)(2,1)}, bf16[10,10,1,32,128]{4,3,2,1,0:T(8,128)(2,1)S(1)}, u32[]{:S(2)}) copy-start(bf16[10,10,1,32,128]{4,3,2,1,0:T(8,128)(2,1)S(1)} %collective-permute-done.4) | copy-start | bytes 2457604
  121.3 152.2 %copy-start.18 = (f32[256,4]{0,1:T(4,128)S(1)}, f32[256,4]{0,1:T(4,128)}, u32[]{:S(2)}) copy-start(f32[256,4]{0,1:T(4,128)} %param.10) | copy-start | bytes 12292
  121.3 152.5 %copy-start.19 = (f32[4,128]{1,0:T(4,128)S(1)}, f32[4,128]{1,0:T(4,128)}, u32[]{:S(2)}) copy-start(f32[4,128]{1,0:T(4,128)} %param.11) | copy-start | bytes 6148
  121.3 149.2 %all-reduce.6.cloned.1.call-start = ((), (), s32[]{:S(2)}) async-start(), calls=%async_computation.3 | async-start | bytes 2097152 | tf_op jit(solution)/shard_map/psum | solution.py:115
  224.3 305.5 %all-reduce.8.cloned.1.call-start = ((), (), s32[]{:S(2)}) async-start(), calls=%async_computation.4 | async-start | bytes 884736 | tf_op jit(solution)/shard_map/psum | solution.py:154
  286.5 23.7 %slice-start.1 = ((s8[8388608]{0:T(1024)(128)(4,1)}), s8[4194304]{0:T(1024)(128)(4,1)S(1)}, s32[]{:S(2)}) async-start(s8[8388608]{0:T(1024)(128)(4,1)} %bitcast.65), calls=%async_computation.6 | async-start | bytes 8388608
  344.1 12.6 %collective-permute-start.6 = (bf16[1,10,6,32,128]{4,3,2,1,0:T(8,128)(2,1)S(1)}, bf16[1,10,6,32,128]{4,3,2,1,0:T(8,128)(2,1)S(1)}, u32[]{:S(2)}, u32[]{:S(2)}) collective-permute-start(bf16[1,10,6,32,128]{4,3,2,1,0:T(8,128)(2,1)S(1)} %get-tuple-element.10), channel_id=1, source_target_pairs={{0,32},{32,64},{64,96},{1,33},{33,65},{65,97},{2,34},{34,66},{66,9... | collective-permute-start | bytes 1474568 | tf_op jit(solution)/shard_map/ppermute | solution.py:26
  346.6 14.1 %collective-permute-start.7 = (bf16[1,10,6,32,128]{4,3,2,1,0:T(8,128)(2,1)S(1)}, bf16[1,10,6,32,128]{4,3,2,1,0:T(8,128)(2,1)S(1)}, u32[]{:S(2)}, u32[]{:S(2)}) collective-permute-start(bf16[1,10,6,32,128]{4,3,2,1,0:T(8,128)(2,1)S(1)} %get-tuple-element.11), channel_id=1, source_target_pairs={{32,0},{64,32},{96,64},{33,1},{65,33},{97,65},{34,2},{66,34},{98,6... | collective-permute-start | bytes 1474568 | tf_op jit(solution)/shard_map/ppermute | solution.py:26
  361.8 25.6 %collective-permute-start.8 = (bf16[8,1,6,32,128]{4,3,2,1,0:T(8,128)(2,1)S(1)}, bf16[8,1,6,32,128]{4,3,2,1,0:T(8,128)(2,1)}, u32[]{:S(2)}, u32[]{:S(2)}) collective-permute-start(bf16[8,1,6,32,128]{4,3,2,1,0:T(8,128)(2,1)S(1)} %get-tuple-element.12), channel_id=1, source_target_pairs={{0,8},{8,16},{16,24},{1,9},{9,17},{17,25},{2,10},{10,18},{18,26},{... | collective-permute-start | bytes 1179656 | tf_op jit(solution)/shard_map/ppermute | solution.py:26
  365.7 21.7 %collective-permute-start.9 = (bf16[8,1,6,32,128]{4,3,2,1,0:T(8,128)(2,1)S(1)}, bf16[8,1,6,32,128]{4,3,2,1,0:T(8,128)(2,1)}, u32[]{:S(2)}, u32[]{:S(2)}) collective-permute-start(bf16[8,1,6,32,128]{4,3,2,1,0:T(8,128)(2,1)S(1)} %get-tuple-element.13), channel_id=1, source_target_pairs={{8,0},{16,8},{24,16},{9,1},{17,9},{25,17},{10,2},{18,10},{26,18},{... | collective-permute-start | bytes 1179656 | tf_op jit(solution)/shard_map/ppermute | solution.py:26
  391.1 144.0 %collective-permute-start.10 = (bf16[8,8,1,32,128]{4,3,2,1,0:T(8,128)(2,1)}, bf16[8,8,1,32,128]{4,3,2,1,0:T(8,128)(2,1)}, u32[]{:S(2)}, u32[]{:S(2)}) collective-permute-start(bf16[8,8,1,32,128]{4,3,2,1,0:T(8,128)(2,1)} %get-tuple-element.16), channel_id=1, source_target_pairs={{0,1},{1,2},{2,3},{3,4},{4,5},{5,6},{6,7},{8,9},{9,10},{10,11},{11... | collective-permute-start | bytes 1572872 | tf_op jit(solution)/shard_map/ppermute | solution.py:26
  394.1 141.0 %collective-permute-start.11 = (bf16[8,8,1,32,128]{4,3,2,1,0:T(8,128)(2,1)}, bf16[8,8,1,32,128]{4,3,2,1,0:T(8,128)(2,1)}, u32[]{:S(2)}, u32[]{:S(2)}) collective-permute-start(bf16[8,8,1,32,128]{4,3,2,1,0:T(8,128)(2,1)} %get-tuple-element.17), channel_id=1, source_target_pairs={{1,0},{2,1},{3,2},{4,3},{5,4},{6,5},{7,6},{9,8},{10,9},{11,10},{12... | collective-permute-start | bytes 1572872 | tf_op jit(solution)/shard_map/ppermute | solution.py:26
  (17 other events, 117.8 us)
Sparse Core Ops, SparseCore 0:
  121.4 102.8 all-reduce.3
  226.7 43.7 all-reduce.5
  383.4 146.3 all-reduce.7
